TPU v7x, 128 devices: a whole 4x4x4 slice. The times are simulated.
128 devices in a mesh: dp: 16 (over x, y), mp: 8 (over z, core).
Axes of the slice: x: 4, y: 4, z: 4, core: 2. Of those that a mesh axis runs over, the one named last changes fastest.
Arguments:
- activations: bfloat16 [16384, 4096], P(('dp', 'mp')), may hold values from -17 to 17
- output_grads: bfloat16 [16384, 14336], P('dp', 'mp'), may hold values from -0.046875 to 0.046875
- q_start: float32 [14336, 64], P('mp'), may hold values from -6 to 6
Outputs:
- new_error: bfloat16 [65536, 14336], P('dp', 'mp')
- q_factor: float32 [14336, 64], P('mp')
All inputs are finite; a program needn't handle non-finite values.
Results may differ from a plain program's by a relative error of at most 0.01.
Values may be sent and summed in bfloat16 or wider, within the bound.
A program may use at most 192 MiB of HBM per device.

v0:
```python
import jax
import jax.numpy as jnp
from jax import lax
from jax.sharding import PartitionSpec as P


def split_up(value, dim, count):
    before, after = (value.shape[:dim], value.shape[dim + 1 :])
    return jnp.moveaxis(value.reshape(*before, count, -1, *after), dim, 0)


def summed_on_arrival(value, axis, dim):
    count = lax.axis_size(axis)
    blocks = lax.all_to_all(split_up(value, dim, count), axis, 0, 0, tiled=True)
    return jnp.sum(blocks, axis=0)


def copy_for_each(value, axis):
    count = lax.axis_size(axis)
    return lax.all_to_all(
        jnp.broadcast_to(value[None], (count, *value.shape)), axis, 0, 0, tiled=True
    )


def taken_together(value, axis):
    return copy_for_each(value, axis).sum(axis=0)


def laid_out(blocks, dim):
    blocks = jnp.moveaxis(blocks, 0, dim)
    shape = blocks.shape
    return blocks.reshape(*shape[:dim], shape[dim] * shape[dim + 1], *shape[dim + 2 :])


def collect(value, axis, dim):
    return laid_out(copy_for_each(value, axis), dim)


def orthonormal(p_mean, gram_matrix):
    lower_tri = jnp.linalg.cholesky(gram_matrix)
    return lax.linalg.triangular_solve(
        lower_tri, p_mean, left_side=False, lower=True, transpose_a=True
    )


def split_parts(values):
    upper = values.astype(jnp.bfloat16)
    lower = (values - upper.astype(jnp.float32)).astype(jnp.bfloat16)
    return (upper, lower)


def per_device(activations, output_grads, q_start):
    contract_rows = (((0,), (0,)), ((), ()))
    replicas = lax.axis_size("dp")
    gathered = lax.all_gather(activations, "mp", axis=0, tiled=True)
    q_upper, q_lower = split_parts(q_start)
    projected = jnp.dot(output_grads, q_upper, preferred_element_type=jnp.float32)
    projected = projected + jnp.dot(output_grads, q_lower, preferred_element_type=jnp.float32)
    proj_upper, proj_lower = split_parts(projected)
    partial_p = lax.dot_general(
        gathered, proj_upper, contract_rows, preferred_element_type=jnp.float32
    )
    partial_p = partial_p + lax.dot_general(
        gathered, proj_lower, contract_rows, preferred_element_type=jnp.float32
    )
    gradient = lax.dot_general(
        gathered, output_grads, contract_rows, preferred_element_type=jnp.float32
    )
    row_block = summed_on_arrival(partial_p, "mp", 0)
    row_block = taken_together(row_block, "dp") / replicas
    block_gram = lax.dot_general(row_block, row_block, contract_rows)
    gram_matrix = taken_together(block_gram, "mp")
    ortho_rows = orthonormal(row_block, gram_matrix)
    p_ortho = collect(ortho_rows, "mp", 0)
    local_factor = lax.dot_general(gradient, p_ortho, contract_rows)
    q_factor = lax.psum(local_factor, "dp") / replicas
    decompressed = lax.dot_general(p_ortho, q_factor, (((1,), (1,)), ((), ())))
    new_error = (gradient - decompressed).astype(jnp.bfloat16)
    return (new_error, q_factor)


def solution(mesh):
    in_specs = (P(("dp", "mp"), None), P("dp", "mp"), P("mp", None))
    out_specs = (P("dp", "mp"), P("mp", None))
    return jax.shard_map(
        per_device, mesh=mesh, in_specs=in_specs, out_specs=out_specs, check_vma=False
    )
```

profile of v0, /device:TPU:0, one launch (start us, length us, event | category | flops | bytes accessed | tf_op | source)
XLA Modules:
  0.0 294.8 jit_solution(3268212242968762611)
XLA Ops:
  7.2 0.7 all-gather.2.cloned.1.call-update
  7.9 3.6 %convolution_bitcast_fusion = f32[1024,64]{0,1:T(8,128)S(1)} fusion(bf16[1024,1792]{1,0:T(8,128)(2,1)} %param.4, f32[1792,64]{0,1:T(8,128)} %param.5), kind=kOutput, calls=%fused_computation.3 | convolution fusion | flops 235339776 | bytes 4390912 | tf_op jit(solution)/shard_map/dot_general | solution.py:58
  11.5 3.4 %convolution_add_fusion.1 = f32[1024,64]{0,1:T(8,128)S(1)} fusion(f32[1024,64]{0,1:T(8,128)S(1)} %convolution_bitcast_fusion, bf16[1024,1792]{1,0:T(8,128)(2,1)} %param.4, f32[1792,64]{0,1:T(8,128)} %param.5), kind=kOutput, calls=%fused_computation.2 | convolution fusion | flops 235061248 | bytes 4653056 | tf_op jit(solution)/shard_map/dot_general | solution.py:57
  14.8 47.3 %all-gather.2.cloned.1.call-done = bf16[1024,4096]{1,0:T(8,128)(2,1)} async-done(((bf16[128,4096]{1,0:T(8,128)(2,1)}), bf16[1024,4096]{1,0:T(8,128)(2,1)}) %all-gather.2.cloned.1.call-update) | async-done | bytes 8388624 | tf_op jit(solution)/shard_map/all_gather | solution.py:55
  62.1 5.1 %fusion.9 = f32[64,4096]{1,0:T(8,128)S(1)} fusion(bf16[1024,4096]{1,0:T(8,128)(2,1)} %all-gather.2.cloned.1.call-done, f32[1024,64]{0,1:T(8,128)S(1)} %convolution_add_fusion.1), kind=kOutput, calls=%fused_computation.17 | convolution fusion | flops 536936448 | bytes 9699328 | tf_op jit(solution)/shard_map/dot_general | solution.py:60
  67.2 0.7 copy-done
  67.9 1.6 convolution_add_fusion
  69.5 19.0 %all_to_all.20 = f32[8,512,64]{1,2,0:T(8,128)S(1)} all-to-all(f32[8,512,64]{1,2,0:T(8,128)S(1)} %bitcast.31), channel_id=1, replica_groups=mesh['dp'=16,'mp'=8] {'mp'}, dimensions={0} | all-to-all | bytes 2097152 | tf_op jit(solution)/shard_map/all_to_all | solution.py:14
  88.8 34.6 %all_to_all.21 = f32[16,512,64]{1,2,0:T(8,128)S(1)} all-to-all(f32[16,512,64]{1,2,0:T(8,128)S(1)} %broadcast_in_dim.7), channel_id=1, replica_groups=mesh['dp'=16,'mp'=8] {'dp'}, dimensions={0} | all-to-all | bytes 4194304 | tf_op jit(solution)/shard_map/all_to_all | solution.py:20
  123.9 8.5 %all_to_all.22 = f32[8,1,4096]{2,1,0:T(1,128)S(1)} all-to-all(f32[8,1,4096]{2,1,0:T(1,128)S(1)} %reshape.24), channel_id=1, replica_groups=mesh['dp'=16,'mp'=8] {'mp'}, dimensions={0} | all-to-all | bytes 262144 | tf_op jit(solution)/shard_map/all_to_all | solution.py:20
  132.4 0.5 broadcast.52
  132.9 1.0 reduce.6
  134.1 5.8 %cholesky.16 = f32[64,64]{1,0:T(8,128)S(1)} custom-call(f32[64,64]{1,0:T(8,128)S(1)} %fusion.13), custom_call_target="Cholesky" | custom-call | tf_op jit(solution)/shard_map/jit(cholesky)/cholesky | solution.py:40
  140.0 0.6 compare_reduce_fusion
  140.7 0.7 fusion.11
  141.3 4.9 %custom-call.6 = f32[1,64,64]{1,2,0:T(8,128)S(1)} custom-call(f32[1,64,64]{2,1,0:T(8,128)S(1)} %fusion.11), custom_call_target="InvertDiagBlocksLowerTriangular" | custom-call | tf_op jit(solution)/shard_map/triangular_solve | solution.py:41
  146.2 0.3 fusion
  146.5 0.8 broadcast_in_dim.10
  147.4 3.5 %all-to-all-start.3 = ((bf16[8,512,64]{1,2,0:T(8,128)(2,1)}), bf16[8,512,64]{1,2,0:T(8,128)(2,1)S(1)}, u32[]{:S(2)}, u32[]{:S(2)}) async-start(bf16[8,512,64]{1,2,0:T(8,128)(2,1)} %broadcast_in_dim.10), calls=%async_computation.3 | async-start | bytes 1048576 | tf_op jit(solution)/shard_map/all_to_all | solution.py:20
  151.1 22.9 %fusion.16 = f32[4096,1792]{1,0:T(8,128)} fusion(bf16[1024,4096]{1,0:T(8,128)(2,1)} %all-gather.2.cloned.1.call-done, bf16[1024,1792]{1,0:T(8,128)(2,1)} %param.4), kind=kOutput, calls=%fused_computation.30 | convolution fusion | flops 15032385536 | bytes 41418752 | tf_op jit(solution)/shard_map/dot_general | solution.py:66
  174.0 12.8 %fusion.17 = f32[1792,64]{0,1:T(8,128)} fusion(f32[4096,1792]{1,0:T(8,128)} %fusion.16, bf16[4096,64]{0,1:T(8,128)(2,1)S(1)} %bitcast.28), kind=kOutput, calls=%fused_computation.31 | convolution fusion | flops 939524096 | bytes 30343168 | tf_op jit(solution)/shard_map/dot_general | solution.py:75
  186.8 82.8 %all-reduce.2.cloned.1.call-done = f32[1792,64]{0,1:T(8,128)} async-done(((f32[1792,64]{0,1:T(8,128)}), f32[1792,64]{0,1:T(8,128)}) %all-reduce.2.cloned.1.call-update) | async-done | bytes 458768 | tf_op jit(solution)/shard_map/psum | solution.py:76
  269.6 1.0 broadcast_multiply_fusion
  270.7 17.3 %subtract_convert_fusion = bf16[4096,1792]{1,0:T(8,128)(2,1)} fusion(f32[4096,1792]{1,0:T(8,128)} %fusion.16, bf16[4096,64]{0,1:T(8,128)(2,1)S(1)} %bitcast.29, f32[1792,64]{0,1:T(8,128)S(1)} %broadcast_multiply_fusion), kind=kOutput, calls=%fused_computation | convolution fusion | flops 954204160 | bytes 45023232 | tf_op jit(solution)/shard_map/dot_general | solution.py:77
  (20 shorter events, 1.5 us)
Async XLA Ops:
  7.2 54.9 %all-gather.2.cloned.1.call-start = ((), (), s32[]{:S(2)}) async-start(), calls=%async_computation.4 | async-start | bytes 9437184 | tf_op jit(solution)/shard_map/all_gather | solution.py:55
  62.1 5.8 %copy-start = (bf16[1024,4096]{1,0:T(8,128)(2,1)S(1)}, bf16[1024,4096]{1,0:T(8,128)(2,1)}, u32[]{:S(2)}) copy-start(bf16[1024,4096]{1,0:T(8,128)(2,1)} %all-gather.2.cloned.1.call-done) | copy-start | bytes 25165828
  147.4 26.6 %all-to-all-start.3 = ((bf16[8,512,64]{1,2,0:T(8,128)(2,1)}), bf16[8,512,64]{1,2,0:T(8,128)(2,1)S(1)}, u32[]{:S(2)}, u32[]{:S(2)}) async-start(bf16[8,512,64]{1,2,0:T(8,128)(2,1)} %broadcast_in_dim.10), calls=%async_computation.3 | async-start | bytes 1048576 | tf_op jit(solution)/shard_map/all_to_all | solution.py:20
  150.9 118.7 %all-reduce.2.cloned.1.call-start = ((), (), s32[]{:S(2)}) async-start(), calls=%async_computation.5 | async-start | bytes 917504 | tf_op jit(solution)/shard_map/psum | solution.py:76
  270.7 17.3 %copy-start.1 = (f32[1792,64]{0,1:T(8,128)}, f32[1792,64]{0,1:T(8,128)S(1)}, u32[]{:S(2)}) copy-start(f32[1792,64]{0,1:T(8,128)S(1)} %broadcast_multiply_fusion) | copy-start | bytes 1376260
Sparse Core Ops, SparseCore 0:
  9.7 52.3 all-gather.1
  186.9 82.6 all-reduce.1
where the time goes:
time: 295 us
  waiting for transfers between devices  131 us (44%)
  matrix products  67 us (23%)
  blocking collectives  62 us (21%)
  other arithmetic  14.3 us (5%)
  between operations  14.2 us (5%)
  starting transfers between devices  3.75 us (1%)
    psum x1, waiting for transfers between devices, per_device(): q_factor = lax.psum(local_factor, 'dp') / replicas  82.8 us
    all_gather x1, waiting for transfers between devices, per_device(): gathered = lax.all_gather(activations, 'mp', axis=0, tiled=True)  47.3 us
    all_to_all x2, blocking collectives, copy_for_each(): lax.all_to_all(jnp.broadcast_to(value[None], (count, *value.shape)), axis...  43.1 us
    dot_general x1, matrix products, per_device(): lax.dot_general(gathered, output_grads, contract_rows, preferred_element_...  22.9 us
    all_to_all x1, blocking collectives, summed_on_arrival(): blocks = lax.all_to_all(split_up(value, dim, count), axis, 0, 0, tiled=True)  19 us
    dot_general x1, matrix products, per_device(): decompressed = lax.dot_general(p_ortho, q_factor, (((1,), (1,)), ((), ())))  17.3 us
    dot_general x1, matrix products, per_device(): local_factor = lax.dot_general(gradient, p_ortho, contract_rows)  12.8 us
    another operation x3, other arithmetic, orthonormal(): lower_tri = jnp.linalg.cholesky(gram_matrix)  6.52 us
  transfers between devices with their start and end apart: 3, of which 2 were waited for; matrix products, arithmetic and copies ran while one was open for 10% of the time, Pallas kernels for 0%

commit v1 on v0

--- a/solution.py
+++ b/solution.py
@@ -52,7 +52,21 @@
 def per_device(activations, output_grads, q_start):
     contract_rows = (((0,), (0,)), ((), ()))
     replicas = lax.axis_size("dp")
-    gathered = lax.all_gather(activations, "mp", axis=0, tiled=True)
+    ways, here, step = (lax.axis_size("mp"), lax.axis_index("mp"), activations.shape[0])
+    shape_2 = [n * ways if d == 0 else n for d, n in enumerate(activations.shape)]
+    full = lax.dynamic_update_slice_in_dim(
+        jnp.zeros(shape_2, activations.dtype), activations, here * step, axis=0
+    )
+    going_up = going_down = activations
+    for far in range(1, ways // 2 + 1):
+        going_up = lax.ppermute(going_up, "mp", [(d, (d + 1) % ways) for d in range(ways)])
+        full = lax.dynamic_update_slice_in_dim(full, going_up, (here - far) % ways * step, axis=0)
+        if 2 * far < ways:
+            going_down = lax.ppermute(going_down, "mp", [(d, (d - 1) % ways) for d in range(ways)])
+            full = lax.dynamic_update_slice_in_dim(
+                full, going_down, (here + far) % ways * step, axis=0
+            )
+    gathered = full
     q_upper, q_lower = split_parts(q_start)
     projected = jnp.dot(output_grads, q_upper, preferred_element_type=jnp.float32)
     projected = projected + jnp.dot(output_grads, q_lower, preferred_element_type=jnp.float32)

time: 295 us -> 307 us (1.041)
  local copies, waits for them, and re-layouts: 2.78 us -> 17.4 us
  waiting for transfers between devices: 131 us -> 117 us
  starting transfers between devices: 3.75 us -> 13.4 us
    all_gather x1 -> x0, waiting for transfers between devices: 47.3 us -> none  [per_device(): gathered = lax.all_gather(activations, 'mp', axis=0, tiled=True)]
    ppermute x0 -> x7, waiting for transfers between devices: none -> 34.4 us  [the longest x4 22.9 us: per_device(): lax.ppermute(going_up, 'mp', [(d, (d + 1) % ways) for d in range(ways)])]
    dynamic_update_slice x0 -> x8, local copies, waits for them, and re-layouts: none -> 10.8 us  [the longest x4 6.65 us: per_device(): lax.dynamic_update_slice_in_dim(full, going_up, (here - far) % ways * ste...]
    ppermute x0 -> x7, starting transfers between devices: none -> 9.7 us  [the longest x3 9.67 us: per_device(): lax.ppermute(going_down, 'mp', [(d, (d - 1) % ways) for d in range(ways)])]
    broadcast_in_dim x0 -> x1, local copies, waits for them, and re-layouts: none -> 4.45 us  [per_device(): jnp.zeros(shape_2, activations.dtype)]
    dot_general x1, matrix products: 1.57 us -> 4.94 us  [per_device(): lax.dot_general(gathered, proj_lower, contract_rows, preferred_element_ty...]
  transfers between devices with their start and end apart: 3 -> 9, of which waited for: 2 -> 7; matrix products, arithmetic and copies ran while one was open for 10% -> 14% of each run, Pallas kernels for 0% -> 0%
where the time goes in v1:
time: 307 us; the launch traced here: 306 us
  waiting for transfers between devices  117 us (38%)
  matrix products  68.1 us (22%)
  blocking collectives  61.7 us (20%)
  local copies, waits for them, and re-layouts  17.4 us (6%)
  other arithmetic  14.3 us (5%)
  between operations  14.3 us (5%)
  starting transfers between devices  13.4 us (4%)
    psum x1, waiting for transfers between devices, per_device(): q_factor = lax.psum(local_factor, 'dp') / replicas  82.7 us
    all_to_all x2, blocking collectives, copy_for_each(): lax.all_to_all(jnp.broadcast_to(value[None], (count, *value.shape)), axis...  43.3 us
    ppermute x4, waiting for transfers between devices, per_device(): lax.ppermute(going_up, 'mp', [(d, (d + 1) % ways) for d in range(ways)])  22.9 us
    dot_general x1, matrix products, per_device(): lax.dot_general(gathered, output_grads, contract_rows, preferred_element_...  22.9 us
    all_to_all x1, blocking collectives, summed_on_arrival(): blocks = lax.all_to_all(split_up(value, dim, count), axis, 0, 0, tiled=True)  18.4 us
    dot_general x1, matrix products, per_device(): decompressed = lax.dot_general(p_ortho, q_factor, (((1,), (1,)), ((), ())))  17.3 us
    dot_general x1, matrix products, per_device(): local_factor = lax.dot_general(gradient, p_ortho, contract_rows)  12.8 us
    ppermute x3, waiting for transfers between devices, per_device(): lax.ppermute(going_down, 'mp', [(d, (d - 1) % ways) for d in range(ways)])  11.5 us
  transfers between devices with their start and end apart: 9, of which 7 were waited for; matrix products, arithmetic and copies ran while one was open for 14% of the time, Pallas kernels for 0%

profile of v1, /device:TPU:0, one launch (start us, length us, event | category | flops | bytes accessed | tf_op | source)
XLA Modules:
  0.0 306.5 jit_solution(5101942436973597551)
XLA Ops:
  7.2 3.6 %collective-permute-start.1 = (bf16[128,4096]{1,0:T(8,128)(2,1)}, bf16[128,4096]{1,0:T(8,128)(2,1)S(1)}, u32[]{:S(2)}, u32[]{:S(2)}) collective-permute-start(bf16[128,4096]{1,0:T(8,128)(2,1)} %param.3), channel_id=1, source_target_pairs={{0,7},{1,0},{2,1},{3,2},{4,3},{5,4},{6,5},{7,6},{8,15},{9,8},{10,9... | collective-permute-start | bytes 3145736 | tf_op jit(solution)/shard_map/ppermute | solution.py:65
  10.8 12.8 %collective-permute-done = bf16[128,4096]{1,0:T(8,128)(2,1)} collective-permute-done((bf16[128,4096]{1,0:T(8,128)(2,1)}, bf16[128,4096]{1,0:T(8,128)(2,1)}, u32[]{:S(2)}, u32[]{:S(2)}) %collective-permute-start) | collective-permute-done | bytes 1048608 | tf_op jit(solution)/shard_map/ppermute | solution.py:62
  23.6 3.6 %convolution_bitcast_fusion = f32[1024,64]{0,1:T(8,128)S(1)} fusion(bf16[1024,1792]{1,0:T(8,128)(2,1)} %param.4, f32[1792,64]{0,1:T(8,128)} %param.5), kind=kOutput, calls=%fused_computation.3 | convolution fusion | flops 235339776 | bytes 4390912 | tf_op jit(solution)/shard_map/dot_general | solution.py:72
  27.2 4.4 %broadcast_in_dim.9 = bf16[1024,4096]{1,0:T(8,128)(2,1)} broadcast(bf16[]{:T(256)} %constant.91.clone.1), dimensions={} | broadcast | bytes 8388610 | tf_op jit(solution)/shard_map/broadcast_in_dim | solution.py:58
  32.7 3.0 collective-permute-start.3
  37.0 2.4 collective-permute-done.2
  39.4 2.3 constant_dynamic-update-slice_fusion.6
  42.7 5.2 %collective-permute-done.3 = bf16[128,4096]{1,0:T(8,128)(2,1)S(1)} collective-permute-done((bf16[128,4096]{1,0:T(8,128)(2,1)S(1)}, bf16[128,4096]{1,0:T(8,128)(2,1)S(1)}, u32[]{:S(2)}, u32[]{:S(2)}) %collective-permute-start.3) | collective-permute-done | bytes 1048608 | tf_op jit(solution)/shard_map/ppermute | solution.py:65
  48.0 3.1 %collective-permute-start.5 = (bf16[128,4096]{1,0:T(8,128)(2,1)S(1)}, bf16[128,4096]{1,0:T(8,128)(2,1)S(1)}, u32[]{:S(2)}, u32[]{:S(2)}) collective-permute-start(bf16[128,4096]{1,0:T(8,128)(2,1)S(1)} %collective-permute-done.3), channel_id=1, source_target_pairs={{0,7},{1,0},{2,1},{3,2},{4,3},{5,4},{6,5},{7,6},{8,15},{9,8},{10,9... | collective-permute-start | bytes 3145736 | tf_op jit(solution)/shard_map/ppermute | solution.py:65
  51.1 2.3 constant_dynamic-update-slice_fusion.4
  57.1 6.3 %collective-permute-done.5 = bf16[128,4096]{1,0:T(8,128)(2,1)S(1)} collective-permute-done((bf16[128,4096]{1,0:T(8,128)(2,1)S(1)}, bf16[128,4096]{1,0:T(8,128)(2,1)S(1)}, u32[]{:S(2)}, u32[]{:S(2)}) %collective-permute-start.5) | collective-permute-done | bytes 1048608 | tf_op jit(solution)/shard_map/ppermute | solution.py:65
  64.4 6.0 %collective-permute-done.6 = bf16[128,4096]{1,0:T(8,128)(2,1)S(1)} collective-permute-done((bf16[128,4096]{1,0:T(8,128)(2,1)S(1)}, bf16[128,4096]{1,0:T(8,128)(2,1)S(1)}, u32[]{:S(2)}, u32[]{:S(2)}) %collective-permute-start.6) | collective-permute-done | bytes 1048608 | tf_op jit(solution)/shard_map/ppermute | solution.py:62
  71.5 4.9 %fusion = f32[4096,64]{0,1:T(8,128)S(1)} fusion(bf16[1024,4096]{1,0:T(8,128)(2,1)} %constant_dynamic-update-slice_fusion, f32[1024,64]{0,1:T(8,128)S(1)} %convolution_add_fusion.1), kind=kOutput, calls=%fused_computation.8 | convolution fusion | flops 537133056 | bytes 9699328 | tf_op jit(solution)/shard_map/dot_general | solution.py:77
  76.4 5.0 %convolution_add_fusion = f32[4096,64]{0,1:T(8,128)S(1)} fusion(f32[4096,64]{0,1:T(8,128)S(1)} %fusion, bf16[1024,4096]{1,0:T(8,128)(2,1)} %constant_dynamic-update-slice_fusion, f32[1024,64]{0,1:T(8,128)S(1)} %convolution_add_fusion.1), kind=kOutput, calls=%fused_computation.1 | convolution fusion | flops 537198592 | bytes 10747904 | tf_op jit(solution)/shard_map/dot_general | solution.py:74
  81.5 18.4 %all_to_all.20 = f32[8,512,64]{1,2,0:T(8,128)S(1)} all-to-all(f32[8,512,64]{1,2,0:T(8,128)S(1)} %bitcast.30), channel_id=1, replica_groups=mesh['dp'=16,'mp'=8] {'mp'}, dimensions={0} | all-to-all | bytes 2097152 | tf_op jit(solution)/shard_map/all_to_all | solution.py:14
  100.3 34.8 %all_to_all.21 = f32[16,512,64]{1,2,0:T(8,128)S(1)} all-to-all(f32[16,512,64]{1,2,0:T(8,128)S(1)} %broadcast_in_dim.11), channel_id=1, replica_groups=mesh['dp'=16,'mp'=8] {'dp'}, dimensions={0} | all-to-all | bytes 4194304 | tf_op jit(solution)/shard_map/all_to_all | solution.py:20
  135.6 8.5 %all_to_all.22 = f32[8,1,4096]{2,1,0:T(1,128)S(1)} all-to-all(f32[8,1,4096]{2,1,0:T(1,128)S(1)} %reshape.24), channel_id=1, replica_groups=mesh['dp'=16,'mp'=8] {'mp'}, dimensions={0} | all-to-all | bytes 262144 | tf_op jit(solution)/shard_map/all_to_all | solution.py:20
  145.8 5.8 %cholesky.16 = f32[64,64]{1,0:T(8,128)S(1)} custom-call(f32[64,64]{1,0:T(8,128)S(1)} %fusion.13), custom_call_target="Cholesky" | custom-call | tf_op jit(solution)/shard_map/jit(cholesky)/cholesky | solution.py:40
  153.0 4.9 %custom-call.6 = f32[1,64,64]{1,2,0:T(8,128)S(1)} custom-call(f32[1,64,64]{2,1,0:T(8,128)S(1)} %fusion.11), custom_call_target="InvertDiagBlocksLowerTriangular" | custom-call | tf_op jit(solution)/shard_map/triangular_solve | solution.py:41
  159.1 3.5 %all-to-all-start.3 = ((bf16[8,512,64]{1,2,0:T(8,128)(2,1)}), bf16[8,512,64]{1,2,0:T(8,128)(2,1)S(1)}, u32[]{:S(2)}, u32[]{:S(2)}) async-start(bf16[8,512,64]{1,2,0:T(8,128)(2,1)} %broadcast_in_dim.13), calls=%async_computation.3 | async-start | bytes 1048576 | tf_op jit(solution)/shard_map/all_to_all | solution.py:20
  162.8 22.9 %fusion.16 = f32[4096,1792]{1,0:T(8,128)} fusion(bf16[1024,4096]{1,0:T(8,128)(2,1)} %constant_dynamic-update-slice_fusion, bf16[1024,1792]{1,0:T(8,128)(2,1)} %param.4), kind=kOutput, calls=%fused_computation.38 | convolution fusion | flops 15032385536 | bytes 41418752 | tf_op jit(solution)/shard_map/dot_general | solution.py:80
  185.7 12.8 %fusion.17 = f32[1792,64]{0,1:T(8,128)} fusion(f32[4096,1792]{1,0:T(8,128)} %fusion.16, bf16[4096,64]{0,1:T(8,128)(2,1)S(1)} %bitcast.27), kind=kOutput, calls=%fused_computation.39 | convolution fusion | flops 939524096 | bytes 30343168 | tf_op jit(solution)/shard_map/dot_general | solution.py:89
  198.5 82.7 %all-reduce.2.cloned.1.call-done = f32[1792,64]{0,1:T(8,128)} async-done(((f32[1792,64]{0,1:T(8,128)}), f32[1792,64]{0,1:T(8,128)}) %all-reduce.2.cloned.1.call-update) | async-done | bytes 458768 | tf_op jit(solution)/shard_map/psum | solution.py:90
  282.3 17.3 %subtract_convert_fusion = bf16[4096,1792]{1,0:T(8,128)(2,1)} fusion(f32[4096,1792]{1,0:T(8,128)} %fusion.16, bf16[4096,64]{0,1:T(8,128)(2,1)S(1)} %bitcast.28, f32[1792,64]{0,1:T(8,128)S(1)} %broadcast_multiply_fusion), kind=kOutput, calls=%fused_computation | convolution fusion | flops 954204160 | bytes 45023232 | tf_op jit(solution)/shard_map/dot_general | solution.py:91
  (44 shorter events, 15.6 us)
Async XLA Ops:
  7.2 24.5 %copy-start.3 = (bf16[128,4096]{1,0:T(8,128)(2,1)S(1)}, bf16[128,4096]{1,0:T(8,128)(2,1)}, u32[]{:S(2)}) copy-start(bf16[128,4096]{1,0:T(8,128)(2,1)} %param.3) | copy-start | bytes 3145732
  7.2 28.5 %copy-start.1 = (f32[1792,64]{0,1:T(8,128)S(1)}, f32[1792,64]{0,1:T(8,128)}, u32[]{:S(2)}) copy-start(f32[1792,64]{0,1:T(8,128)} %param.5) | copy-start | bytes 1376260
  7.2 16.4 %collective-permute-start = (bf16[128,4096]{1,0:T(8,128)(2,1)}, bf16[128,4096]{1,0:T(8,128)(2,1)}, u32[]{:S(2)}, u32[]{:S(2)}) collective-permute-start(bf16[128,4096]{1,0:T(8,128)(2,1)} %param.3), channel_id=1, source_target_pairs={{0,1},{1,2},{2,3},{3,4},{4,5},{5,6},{6,7},{7,0},{8,9},{9,10},{10,1... | collective-permute-start | bytes 3145736 | tf_op jit(solution)/shard_map/ppermute | solution.py:62
  7.2 25.5 %collective-permute-start.1 = (bf16[128,4096]{1,0:T(8,128)(2,1)}, bf16[128,4096]{1,0:T(8,128)(2,1)S(1)}, u32[]{:S(2)}, u32[]{:S(2)}) collective-permute-start(bf16[128,4096]{1,0:T(8,128)(2,1)} %param.3), channel_id=1, source_target_pairs={{0,7},{1,0},{2,1},{3,2},{4,3},{5,4},{6,5},{7,6},{8,15},{9,8},{10,9... | collective-permute-start | bytes 3145736 | tf_op jit(solution)/shard_map/ppermute | solution.py:65
  10.8 24.8 %copy-start = (bf16[1024,1792]{1,0:T(8,128)(2,1)S(1)}, bf16[1024,1792]{1,0:T(8,128)(2,1)}, u32[]{:S(2)}) copy-start(bf16[1024,1792]{1,0:T(8,128)(2,1)} %param.4) | copy-start | bytes 11010052
  23.6 15.8 %collective-permute-start.2 = (bf16[128,4096]{1,0:T(8,128)(2,1)}, bf16[128,4096]{1,0:T(8,128)(2,1)}, u32[]{:S(2)}, u32[]{:S(2)}) collective-permute-start(bf16[128,4096]{1,0:T(8,128)(2,1)} %collective-permute-done), channel_id=1, source_target_pairs={{0,1},{1,2},{2,3},{3,4},{4,5},{5,6},{6,7},{7,0},{8,9},{9,10},{10,1... | collective-permute-start | bytes 3145736 | tf_op jit(solution)/shard_map/ppermute | solution.py:62
  32.7 15.3 %collective-permute-start.3 = (bf16[128,4096]{1,0:T(8,128)(2,1)S(1)}, bf16[128,4096]{1,0:T(8,128)(2,1)S(1)}, u32[]{:S(2)}, u32[]{:S(2)}) collective-permute-start(bf16[128,4096]{1,0:T(8,128)(2,1)S(1)} %collective-permute-done.1), channel_id=1, source_target_pairs={{0,7},{1,0},{2,1},{3,2},{4,3},{5,4},{6,5},{7,6},{8,15},{9,8},{10,9... | collective-permute-start | bytes 3145736 | tf_op jit(solution)/shard_map/ppermute | solution.py:65
  39.4 15.6 %collective-permute-start.4 = (bf16[128,4096]{1,0:T(8,128)(2,1)}, bf16[128,4096]{1,0:T(8,128)(2,1)S(1)}, u32[]{:S(2)}, u32[]{:S(2)}) collective-permute-start(bf16[128,4096]{1,0:T(8,128)(2,1)} %collective-permute-done.2), channel_id=1, source_target_pairs={{0,1},{1,2},{2,3},{3,4},{4,5},{5,6},{6,7},{7,0},{8,9},{9,10},{10,1... | collective-permute-start | bytes 3145736 | tf_op jit(solution)/shard_map/ppermute | solution.py:62
  48.0 15.4 %collective-permute-start.5 = (bf16[128,4096]{1,0:T(8,128)(2,1)S(1)}, bf16[128,4096]{1,0:T(8,128)(2,1)S(1)}, u32[]{:S(2)}, u32[]{:S(2)}) collective-permute-start(bf16[128,4096]{1,0:T(8,128)(2,1)S(1)} %collective-permute-done.3), channel_id=1, source_target_pairs={{0,7},{1,0},{2,1},{3,2},{4,3},{5,4},{6,5},{7,6},{8,15},{9,8},{10,9... | collective-permute-start | bytes 3145736 | tf_op jit(solution)/shard_map/ppermute | solution.py:65
  55.0 15.4 %collective-permute-start.6 = (bf16[128,4096]{1,0:T(8,128)(2,1)S(1)}, bf16[128,4096]{1,0:T(8,128)(2,1)S(1)}, u32[]{:S(2)}, u32[]{:S(2)}) collective-permute-start(bf16[128,4096]{1,0:T(8,128)(2,1)S(1)} %collective-permute-done.4), channel_id=1, source_target_pairs={{0,1},{1,2},{2,3},{3,4},{4,5},{5,6},{6,7},{7,0},{8,9},{9,10},{10,1... | collective-permute-start | bytes 3145736 | tf_op jit(solution)/shard_map/ppermute | solution.py:62
  159.1 26.6 %all-to-all-start.3 = ((bf16[8,512,64]{1,2,0:T(8,128)(2,1)}), bf16[8,512,64]{1,2,0:T(8,128)(2,1)S(1)}, u32[]{:S(2)}, u32[]{:S(2)}) async-start(bf16[8,512,64]{1,2,0:T(8,128)(2,1)} %broadcast_in_dim.13), calls=%async_computation.3 | async-start | bytes 1048576 | tf_op jit(solution)/shard_map/all_to_all | solution.py:20
  162.6 118.7 %all-reduce.2.cloned.1.call-start = ((), (), s32[]{:S(2)}) async-start(), calls=%async_computation.4 | async-start | bytes 917504 | tf_op jit(solution)/shard_map/psum | solution.py:90
  282.3 17.3 %copy-start.2 = (f32[1792,64]{0,1:T(8,128)}, f32[1792,64]{0,1:T(8,128)S(1)}, u32[]{:S(2)}) copy-start(f32[1792,64]{0,1:T(8,128)S(1)} %broadcast_multiply_fusion) | copy-start | bytes 1376260
Sparse Core Ops, SparseCore 0:
  198.7 82.5 all-reduce.1
